TPU v7x, 128 devices: a whole 4x4x4 slice. The times are simulated.
128 devices in a mesh: seq: 8 (over x, core), tp: 16 (over y, z).
Axes of the slice: x: 4, y: 4, z: 4, core: 2. Of those that a mesh axis runs over, the one named last changes fastest.
Arguments:
- vit_input: bfloat16 [8192, 1280], P(('seq', 'tp')), may hold values from -6 to 6
- image_lengths: int32 [8, 2], P('seq'), may hold values from 1 to 192, 256 in all within a row
- positions: int32 [2048], replicated, may hold values from 0 to 2047, each once
- vit_ln_gain: float32 [1280], replicated, may hold values from 0.25 to 1.75
- w_qkv: bfloat16 [1280, 3, 1280], P(None, None, 'tp'), may hold values from -0.15625 to 0.15625
- w_proj: bfloat16 [1280, 1280], P('tp'), may hold values from -0.15625 to 0.15625
- merger_ln_gain: float32 [1280], replicated, may hold values from 0.25 to 1.75
- merger_w1: bfloat16 [5120, 5120], P(None, 'tp'), may hold values from -0.078125 to 0.078125
- merger_w2: bfloat16 [5120, 8192], P('tp'), may hold values from -0.36336105 to 0.36336105
- norm_gain: float32 [8192], P('seq'), may hold values from 0.25 to 1.75
- gate_up_weight: bfloat16 [8192, 2, 29568], P('seq', None, 'tp'), may hold values from -0.0625 to 0.0625
- down_weight: bfloat16 [29568, 8192], P('tp', 'seq'), may hold values from -0.125 to 0.125
Outputs:
- mixed: bfloat16 [2048, 8192], P('tp', 'seq')
Inputs may be any that keep to these rules, and one draw needn't show every extreme that they name: `image_lengths`: each row sums to 256. `positions`: a permutation: every slot once.
All inputs are finite; a program needn't handle non-finite values.
Results may differ from a plain program's by a relative error of at most 0.038.
Values may be sent and summed in bfloat16 or wider, within the bound.
A program may use at most 128 MiB of HBM per device.

v0:
```python
import jax
import jax.numpy as jnp
from jax import lax
from jax.sharding import Mesh
from jax.sharding import PartitionSpec as P

D = 8192
HD = 80
TP = ("tp_0", "tp_1")
SEQ_TP = ("seq", "tp_0", "tp_1")


def from_everyone(x, axis):
    copies = jnp.broadcast_to(x, (lax.axis_size(axis), *x.shape))
    return lax.all_to_all(copies, axis, split_axis=0, concat_axis=0, tiled=True)


def laid_out(tiles, dim):
    shape = list(tiles.shape[1:])
    shape[dim] *= tiles.shape[0]
    return jnp.moveaxis(tiles, 0, dim).reshape(shape)


def gathered_copies(x, axis, dim):
    tiles = from_everyone(x, axis)
    return laid_out(tiles, dim)


def cut_along(x, dim, devices):
    before, after = (x.shape[:dim], x.shape[dim + 1 :])
    return jnp.moveaxis(x.reshape(*before, devices, -1, *after), dim, 0)


def sum_at_owner(x, axis, dim):
    devices = lax.axis_size(axis)
    tiles = lax.all_to_all(cut_along(x, dim, devices), axis, 0, 0, tiled=True)
    return jnp.sum(tiles.astype(jnp.float32), axis=0)


def over_copies(x, axis):
    everything = from_everyone(x, axis)
    return jnp.sum(everything, axis=0)


def sum_by_axis(x, axes, dim):
    if not axes:
        return x
    nearer = lax.psum_scatter(x, axes[0], scatter_dimension=dim, tiled=True)
    return sum_by_axis(nearer, axes[1:], dim)


def layer_norm(values, gain):
    mean = jnp.mean(values, axis=-1, keepdims=True)
    centered = values - mean
    variance = jnp.mean(centered * centered, axis=-1, keepdims=True)
    return centered * lax.rsqrt(variance + 1e-06) * gain


def image_ids(lengths, count):
    image_ends = jnp.cumsum(lengths) * 4
    patch_index = jnp.arange(count, dtype=jnp.int32)
    return jnp.sum((patch_index[:, None] >= image_ends[None, :]).astype(jnp.int32), axis=1)


def attend(query, keys, values, image_index):
    scores = jnp.einsum("qhe,khe->hqk", query, keys, preferred_element_type=jnp.float32) * HD ** (
        -0.5
    )
    same_image = image_index[:, None] == image_index[None, :]
    scores = jnp.where(same_image[None], scores, -1e30)
    top = jnp.max(scores, axis=-1, keepdims=True)
    expo = jnp.exp(scores - top)
    weights = (expo / jnp.sum(expo, axis=-1, keepdims=True)).astype(jnp.bfloat16)
    output = jnp.einsum("hqk,khe->qhe", weights, values, preferred_element_type=jnp.float32)
    return output.astype(jnp.bfloat16)


def slot_sources(positions):
    count = positions.shape[0]
    return jnp.zeros((count,), jnp.int32).at[positions].set(jnp.arange(count, dtype=jnp.int32))


def local(
    vit_input,
    image_lengths,
    positions,
    vit_ln_gain,
    w_qkv,
    w_proj,
    merger_ln_gain,
    merger_w1,
    merger_w2,
    norm_gain,
    gate_up_weight,
    down_weight,
):
    tp_size = lax.axis_size(TP)
    seq_size = lax.axis_size("seq")
    own_patches = vit_input.shape[0]
    patch_width = vit_input.shape[1]
    head_cols = w_qkv.shape[2]
    local_heads = head_cols // HD
    normed_patches = layer_norm(vit_input.astype(jnp.float32), vit_ln_gain).astype(jnp.bfloat16)
    w_qkv_flat = w_qkv.reshape(patch_width, 3 * head_cols)
    projected = jnp.dot(
        gathered_copies(normed_patches, TP, 0), w_qkv_flat, preferred_element_type=jnp.float32
    ).astype(jnp.bfloat16)
    group_patches = projected.shape[0]
    projected = projected.reshape(group_patches, 3, local_heads, HD)
    image_index = image_ids(image_lengths[0], group_patches)
    attended = attend(projected[:, 0], projected[:, 1], projected[:, 2], image_index).reshape(
        group_patches, head_cols
    )
    picked = attended
    attn_sum = sum_at_owner(
        jnp.dot(picked, w_proj, preferred_element_type=jnp.float32).astype(jnp.bfloat16), TP, 0
    )
    vit_out = vit_input.astype(jnp.float32) + attn_sum
    own_tokens = own_patches // 4
    merged_in = (
        layer_norm(vit_out, merger_ln_gain)
        .astype(jnp.bfloat16)
        .reshape(own_tokens, 4 * patch_width)
    )
    expanded = jax.nn.gelu(
        jnp.dot(gathered_copies(merged_in, TP, 0), merger_w1, preferred_element_type=jnp.float32),
        approximate=False,
    ).astype(jnp.bfloat16)
    picked = expanded
    vis_rows = sum_at_owner(
        jnp.dot(picked, merger_w2, preferred_element_type=jnp.float32).astype(jnp.bfloat16), TP, 0
    ).astype(jnp.bfloat16)
    blocks = lax.all_to_all(vis_rows, "seq", split_axis=1, concat_axis=0, tiled=True)
    gathered = lax.all_gather(blocks, TP, axis=0, tiled=True)
    col_width = gathered.shape[1]
    all_tokens = (
        gathered.reshape(tp_size, seq_size, own_tokens, col_width)
        .transpose(1, 0, 2, 3)
        .reshape(tp_size * seq_size * own_tokens, col_width)
    )
    seq_rows = all_tokens.shape[0]
    seq_tokens = jnp.take(all_tokens, slot_sources(positions), axis=0)
    token_values = seq_tokens.astype(jnp.float32)
    row_squares = over_copies(jnp.sum(token_values * token_values, axis=1), "seq")
    inverse_rms = lax.rsqrt(row_squares / D + 1e-06)
    normed = (token_values * inverse_rms[:, None] * norm_gain).astype(jnp.bfloat16)
    slice_width = seq_tokens.shape[1]
    hidden_width = gate_up_weight.shape[2]
    weight_flat = gate_up_weight.reshape(slice_width, 2 * hidden_width)
    out_rows = seq_rows // tp_size
    picked = normed
    gate_up = lax.psum_scatter(
        jnp.dot(picked, weight_flat, preferred_element_type=jnp.float32).astype(jnp.bfloat16),
        "seq",
        scatter_dimension=0,
        tiled=True,
    ).astype(jnp.float32)
    hidden = (jax.nn.silu(gate_up[:, :hidden_width]) * gate_up[:, hidden_width:]).astype(
        jnp.bfloat16
    )
    terms = jnp.dot(
        lax.all_gather(hidden, "seq", axis=0, tiled=True),
        down_weight,
        preferred_element_type=jnp.float32,
    )
    down_sum = sum_by_axis(terms.astype(jnp.bfloat16), TP, 0).astype(jnp.float32)
    residual = lax.dynamic_slice_in_dim(token_values, lax.axis_index(TP) * out_rows, out_rows, 0)
    return (residual + down_sum).astype(jnp.bfloat16)


def solution(mesh):
    finer = Mesh(mesh.devices.reshape(mesh.shape["seq"], 4, 4), ("seq", "tp_0", "tp_1"))
    in_specs = (
        P(SEQ_TP, None),
        P("seq", None),
        P(),
        P(),
        P(None, None, TP),
        P(TP, None),
        P(),
        P(None, TP),
        P(TP, None),
        P("seq"),
        P("seq", None, TP),
        P(TP, "seq"),
    )
    out_specs = P(TP, "seq")
    return jax.shard_map(local, mesh=finer, in_specs=in_specs, out_specs=out_specs, check_vma=False)
```

profile of v0, /device:TPU:0, one launch (start us, length us, event | category | flops | bytes accessed | tf_op | source)
XLA Modules:
  0.0 555.1 jit_solution(18318716780304703547)
XLA Ops:
  11.7 8.2 %all-to-all-start = ((bf16[16,64,1280]{2,1,0:T(8,128)(2,1)}), bf16[16,64,1280]{2,1,0:T(8,128)(2,1)}, u32[]{:S(2)}, u32[]{:S(2)}) async-start(bf16[16,64,1280]{2,1,0:T(8,128)(2,1)} %broadcast_in_dim.26), calls=%async_computation | async-start | bytes 5242880 | tf_op jit(solution)/shard_map/all_to_all | solution.py:15
  20.3 36.8 %all-to-all-done = bf16[16,64,1280]{2,1,0:T(8,128)(2,1)} async-done(((bf16[16,64,1280]{2,1,0:T(8,128)(2,1)}), bf16[16,64,1280]{2,1,0:T(8,128)(2,1)}, u32[]{:S(2)}, u32[]{:S(2)}) %all-to-all-start) | async-done | bytes 2621472 | tf_op jit(solution)/shard_map/all_to_all | solution.py:15
  57.1 2.7 convolution_convert_fusion.4
  60.7 1.9 copy-done.3
  63.6 6.0 %convolution_convert_fusion.2 = bf16[1024,1280]{1,0:T(8,128)(2,1)} fusion(bf16[80,1280]{1,0:T(8,128)(2,1)S(1)} %copy-done.6, f32[1024,1024]{0,1:T(8,128)} %copy-done.3, f32[1024]{0:T(1024)S(1)} %fusion.3, f32[1024]{0:T(1024)S(1)} %get-tuple-element.5, s32[1024]{0:T(1024)S(1)} %fusion.57, bf16[1024,3,1,80]{0,3,1,2:T(8,128)(2,1)} %bitcast.64), kind=kOutput, calls=%fused_computation.14 | convolution fusion | flops 385171456 | bytes 7200768 | tf_op jit(solution)/shard_map/dot_general | solution.py:116
  69.6 37.0 %all_to_all.45 = bf16[16,64,1280]{2,1,0:T(8,128)(2,1)S(1)} all-to-all(bf16[16,64,1280]{2,1,0:T(8,128)(2,1)} %bitcast.55), channel_id=1, replica_groups=mesh['seq'=8,'tp_0'=4,'tp_1'=4] {'tp_0','tp_1'}, dimensions={0} | all-to-all | bytes 5242880 | tf_op jit(solution)/shard_map/all_to_all | solution.py:36
  109.5 35.3 %all_to_all.46 = bf16[16,16,5120]{2,1,0:T(8,128)(2,1)} all-to-all(bf16[16,16,5120]{2,1,0:T(8,128)(2,1)S(1)} %broadcast_in_dim.47), channel_id=1, replica_groups=mesh['seq'=8,'tp_0'=4,'tp_1'=4] {'tp_0','tp_1'}, dimensions={0} | all-to-all | bytes 5242880 | tf_op jit(solution)/shard_map/all_to_all | solution.py:15
  144.8 10.9 %convolution_convert_fusion.1 = bf16[256,8192]{1,0:T(8,128)(2,1)} fusion(bf16[320,8192]{1,0:T(8,128)(2,1)} %param.20, bf16[256,5120]{1,0:T(8,128)(2,1)} %bitcast.56, bf16[5120,320]{0,1:T(8,128)(2,1)S(1)} %copy-done), kind=kOutput, calls=%fused_computation.3 | convolution fusion | flops 2188460032 | bytes 15335424 | tf_op jit(solution)/shard_map/dot_general | solution.py:131
  155.7 51.6 %all_to_all.47 = bf16[16,16,8192]{2,1,0:T(8,128)(2,1)} all-to-all(bf16[16,16,8192]{2,1,0:T(8,128)(2,1)} %bitcast.54), channel_id=1, replica_groups=mesh['seq'=8,'tp_0'=4,'tp_1'=4] {'tp_0','tp_1'}, dimensions={0} | all-to-all | bytes 8388608 | tf_op jit(solution)/shard_map/all_to_all | solution.py:36
  207.3 2.9 reduce_sum.100
  210.2 11.7 %all_to_all.48 = bf16[16,8,1024]{2,0,1:T(8,128)(2,1)} all-to-all(bf16[16,8,1024]{2,0,1:T(8,128)(2,1)S(1)} %bitcast.59), channel_id=1, replica_groups=mesh['seq'=8,'tp_0'=4,'tp_1'=4] {'seq'}, dimensions={1} | all-to-all | bytes 524288 | tf_op jit(solution)/shard_map/all_to_all | solution.py:133
  222.0 8.0 %scatter_custom_fusion = s32[2048]{0:T(1024)S(1)} fusion(s32[2048]{0:T(1024)S(1)} %compare_select_fusion.1, s32[2048]{0:T(1024)S(1)} %iota.7, s32[]{:T(128)} %constant.45.clone.1), kind=kCustom, calls=%fused_computation.97 | custom fusion | bytes 8196 | tf_op jit(solution)/shard_map/scatter | solution.py:80
  230.1 39.4 %all-gather.3.cloned.1.call-done = bf16[2048,1024]{1,0:T(8,128)(2,1)} async-done(((bf16[128,1024]{1,0:T(8,128)(2,1)}), bf16[2048,1024]{1,0:T(8,128)(2,1)}) %all-gather.3.cloned.1.call-update) | async-done | bytes 4194320 | tf_op jit(solution)/shard_map/all_gather | solution.py:134
  269.6 5.0 copy.21
  274.6 13.7 %gather_fusion = bf16[2048,1024]{1,0:T(8,128)(2,1)} fusion(bf16[2048,1024]{1,0:T(8,128)(2,1)} %bitcast.52, s32[2048]{0:T(1024)S(1)} %fusion.58), kind=kCustom, calls=%fused_computation | custom fusion | bytes 8396800 | tf_op jit(solution)/shard_map/jit(_take)/gather | solution.py:142
  288.2 3.1 multiply_reduce_fusion
  291.4 9.7 %all_to_all.49 = f32[8,1,2048]{2,1,0:T(1,128)S(1)} all-to-all(f32[8,1,2048]{2,1,0:T(1,128)S(1)} %broadcast_in_dim.50), channel_id=1, replica_groups=mesh['seq'=8,'tp_0'=4,'tp_1'=4] {'seq'}, dimensions={0} | all-to-all | bytes 131072 | tf_op jit(solution)/shard_map/all_to_all | solution.py:15
  301.1 22.3 %convolution_convert_fusion = bf16[2048,3696]{0,1:T(8,128)(2,1)} fusion(bf16[1024,3696]{0,1:T(8,128)(2,1)} %bitcast.60, f32[1024]{0:T(1024)S(1)} %copy-done.7, f32[2048]{0:T(1024)S(1)} %add_rsqrt_fusion, bf16[2048,1024]{1,0:T(8,128)(2,1)} %gather_fusion, pred[2048]{0:T(1024)(128)(4,1)S(1)} %compare_and_fusion), kind=kOutput, calls=%fused_computation.2 | convolution fusion | flops 15520202752 | bytes 26916864 | tf_op jit(solution)/shard_map/dot_general | solution.py:153
  323.5 82.4 %reduce-scatter.4.cloned.1.call-done = bf16[256,3696]{0,1:T(8,128)(2,1)} async-done(((bf16[2048,3696]{0,1:T(8,128)(2,1)}), bf16[256,3696]{0,1:T(8,128)(2,1)}) %reduce-scatter.4.cloned.1.call-update) | async-done | bytes 1892368 | tf_op jit(solution)/shard_map/reduce_scatter | solution.py:152
  409.4 49.6 %all-gather.5.cloned.1.call-done = bf16[2048,1848]{0,1:T(8,128)(2,1)} async-done(((bf16[256,1848]{0,1:T(8,128)(2,1)}), bf16[2048,1848]{0,1:T(8,128)(2,1)}) %all-gather.5.cloned.1.call-update) | async-done | bytes 7569424 | tf_op jit(solution)/shard_map/all_gather | solution.py:162
  459.0 13.7 %convolution_convert_fusion.3 = bf16[2048,1024]{1,0:T(8,128)(2,1)} fusion(bf16[2048,1848]{0,1:T(8,128)(2,1)} %all-gather.5.cloned.1.call-done, bf16[1848,1024]{1,0:T(8,128)(2,1)} %param.23), kind=kOutput, calls=%fused_computation.15 | convolution fusion | flops 7753170944 | bytes 15548416 | tf_op jit(solution)/shard_map/dot_general | solution.py:161
  472.8 47.9 %reduce-scatter.6.cloned.1.call-done = bf16[512,1024]{1,0:T(8,128)(2,1)} async-done(((bf16[2048,1024]{1,0:T(8,128)(2,1)}), bf16[512,1024]{1,0:T(8,128)(2,1)}) %reduce-scatter.6.cloned.1.call-update) | async-done | bytes 1048592 | tf_op jit(solution)/shard_map/reduce_scatter | solution.py:48
  520.8 5.3 fusion.95
  526.1 20.6 %reduce-scatter.8.cloned.1.call-done = bf16[128,1024]{1,0:T(8,128)(2,1)} async-done(((bf16[512,1024]{1,0:T(8,128)(2,1)}), bf16[128,1024]{1,0:T(8,128)(2,1)}) %reduce-scatter.8.cloned.1.call-update) | async-done | bytes 262160 | tf_op jit(solution)/shard_map/reduce_scatter | solution.py:48
  (59 shorter events, 15.8 us)
Async XLA Ops:
  6.5 138.2 %copy-start = (bf16[5120,320]{0,1:T(8,128)(2,1)S(1)}, bf16[5120,320]{0,1:T(8,128)(2,1)}, u32[]{:S(2)}) copy-start(bf16[5120,320]{0,1:T(8,128)(2,1)} %param.19) | copy-start | bytes 9830404
  8.9 11.1 %copy-start.8 = (s32[1,2]{1,0:T(1,128)S(1)}, s32[1,2]{1,0:T(1,128)}, u32[]{:S(2)}) copy-start(s32[1,2]{1,0:T(1,128)} %param.13) | copy-start | bytes 28
  11.7 45.3 %all-to-all-start = ((bf16[16,64,1280]{2,1,0:T(8,128)(2,1)}), bf16[16,64,1280]{2,1,0:T(8,128)(2,1)}, u32[]{:S(2)}, u32[]{:S(2)}) async-start(bf16[16,64,1280]{2,1,0:T(8,128)(2,1)} %broadcast_in_dim.26), calls=%async_computation | async-start | bytes 5242880 | tf_op jit(solution)/shard_map/all_to_all | solution.py:15
  19.9 249.6 %all-gather.3.cloned.1.call-start = ((), (), s32[]{:S(2)}) async-start(), calls=%async_computation.9 | async-start | bytes 4456448 | tf_op jit(solution)/shard_map/all_gather | solution.py:134
  59.8 0.9 copy-start.9
  59.8 3.8 copy-start.6
  60.7 1.9 copy-start.3
  69.6 37.4 %copy-start.2 = (bf16[64,1280]{1,0:T(8,128)(2,1)S(1)}, bf16[64,1280]{1,0:T(8,128)(2,1)}, u32[]{:S(2)}) copy-start(bf16[64,1280]{1,0:T(8,128)(2,1)} %param.12) | copy-start | bytes 491524
  69.6 37.7 %copy-start.5 = (f32[1280]{0:T(1024)S(1)}, f32[1280]{0:T(1024)}, u32[]{:S(2)}) copy-start(f32[1280]{0:T(1024)} %param.18) | copy-start | bytes 15364
  207.3 14.7 %copy-start.4 = (s32[2048]{0:T(1024)S(1)}, s32[2048]{0:T(1024)}, u32[]{:S(2)}) copy-start(s32[2048]{0:T(1024)} %param.14) | copy-start | bytes 24580
  222.0 184.0 %reduce-scatter.4.cloned.1.call-start = ((), (), s32[]{:S(2)}) async-start(), calls=%async_computation.10 | async-start | bytes 17031168 | tf_op jit(solution)/shard_map/reduce_scatter | solution.py:152
  288.2 12.9 %copy-start.7 = (f32[1024]{0:T(1024)S(1)}, f32[1024]{0:T(1024)}, u32[]{:S(2)}) copy-start(f32[1024]{0:T(1024)} %param.21) | copy-start | bytes 12292
  323.5 135.5 %all-gather.5.cloned.1.call-start = ((), (), s32[]{:S(2)}) async-start(), calls=%async_computation.11 | async-start | bytes 8515584 | tf_op jit(solution)/shard_map/all_gather | solution.py:162
  409.3 111.4 %reduce-scatter.6.cloned.1.call-start = ((), (), s32[]{:S(2)}) async-start(), calls=%async_computation.12 | async-start | bytes 5242880 | tf_op jit(solution)/shard_map/reduce_scatter | solution.py:48
  472.7 74.0 %reduce-scatter.8.cloned.1.call-start = ((), (), s32[]{:S(2)}) async-start(), calls=%async_computation.13 | async-start | bytes 1310720 | tf_op jit(solution)/shard_map/reduce_scatter | solution.py:48
  520.7 27.8 %copy-start.1 = (bf16[5120,320]{0,1:T(8,128)(2,1)S(1)}, bf16[5120,320]{0,1:T(8,128)(2,1)}, u32[]{:S(2)}) copy-start(bf16[5120,320]{0,1:T(8,128)(2,1)} %param.19) | copy-start | bytes 9830404
Sparse Core Ops, SparseCore 0:
  222.1 47.4 all-gather.2
  323.6 82.2 reduce-scatter.3
  409.4 49.4 all-gather.4
  472.9 47.8 reduce-scatter.5
  523.0 23.6 reduce-scatter.7
where the time goes:
time: 556 us; the launch traced here: 555 us
  waiting for transfers between devices  277 us (50%)
  blocking collectives  145 us (26%)
  matrix products  56.6 us (10%)
  local copies, waits for them, and re-layouts  32.5 us (6%)
  other arithmetic  22.1 us (4%)
  between operations  13.4 us (2%)
  starting transfers between devices  8.41 us (2%)
    all_to_all x2, blocking collectives, sum_at_owner(): tiles = lax.all_to_all(cut_along(x, dim, devices), axis, 0, 0, tiled=True)  88.6 us
    reduce_scatter x1, waiting for transfers between devices, local(): lax.psum_scatter(jnp.dot(picked, weight_flat, preferred_element_type=jnp....  82.4 us
    reduce_scatter x2, waiting for transfers between devices, sum_by_axis(): nearer = lax.psum_scatter(x, axes[0], scatter_dimension=dim, tiled=True)  68.6 us
    all_gather x1, waiting for transfers between devices, local(): lax.all_gather(hidden, 'seq', axis=0, tiled=True)  49.6 us
    all_to_all x2, blocking collectives, from_everyone(): return lax.all_to_all(copies, axis, split_axis=0, concat_axis=0, tiled=True)  45 us
    all_gather x1, waiting for transfers between devices, local(): gathered = lax.all_gather(blocks, TP, axis=0, tiled=True)  39.4 us
    all_to_all x1, waiting for transfers between devices, from_everyone(): return lax.all_to_all(copies, axis, split_axis=0, concat_axis=0, tiled=True)  36.8 us
    dot_general x1, matrix products, local(): jnp.dot(picked, weight_flat, preferred_element_type=jnp.float32)  22.3 us
  transfers between devices with their start and end apart: 6, of which 6 were waited for; matrix products, arithmetic and copies ran while one was open for 2% of the time, Pallas kernels for 0%

commit v1 on v0

--- a/solution.py
+++ b/solution.py
@@ -8,6 +8,27 @@
 HD = 80
 TP = ("tp_0", "tp_1")
 SEQ_TP = ("seq", "tp_0", "tp_1")
+
+
+def collect(x, axis, dim):
+    devices, index, rows = (lax.axis_size(axis), lax.axis_index(axis), x.shape[dim])
+    upward = [(i, (i + 1) % devices) for i in range(devices)]
+    left = [(i, (i - 1) % devices) for i in range(devices)]
+    result = jnp.zeros((*x.shape[:dim], devices * rows, *x.shape[dim + 1 :]), x.dtype)
+    result = lax.dynamic_update_slice_in_dim(result, x, index * rows, axis=dim)
+    from_left = from_right = x
+    halfway = devices // 2
+    for step in range(1, halfway + 1):
+        from_left = lax.ppermute(from_left, axis, upward)
+        result = lax.dynamic_update_slice_in_dim(
+            result, from_left, (index - step) % devices * rows, axis=dim
+        )
+        if step < devices - halfway:
+            from_right = lax.ppermute(from_right, axis, left)
+            result = lax.dynamic_update_slice_in_dim(
+                result, from_right, (index + step) % devices * rows, axis=dim
+            )
+    return result
 
 
 def from_everyone(x, axis):
@@ -158,11 +179,7 @@
     hidden = (jax.nn.silu(gate_up[:, :hidden_width]) * gate_up[:, hidden_width:]).astype(
         jnp.bfloat16
     )
-    terms = jnp.dot(
-        lax.all_gather(hidden, "seq", axis=0, tiled=True),
-        down_weight,
-        preferred_element_type=jnp.float32,
-    )
+    terms = jnp.dot(collect(hidden, "seq", 0), down_weight, preferred_element_type=jnp.float32)
     down_sum = sum_by_axis(terms.astype(jnp.bfloat16), TP, 0).astype(jnp.float32)
     residual = lax.dynamic_slice_in_dim(token_values, lax.axis_index(TP) * out_rows, out_rows, 0)
     return (residual + down_sum).astype(jnp.bfloat16)

time: 556 us -> 565 us (1.016)
  local copies, waits for them, and re-layouts: 32.5 us -> 46.4 us
  waiting for transfers between devices: 277 us -> 265 us
  starting transfers between devices: 8.41 us -> 17.4 us
    all_gather x1 -> x0, waiting for transfers between devices: 49.6 us -> none  [local(): lax.all_gather(hidden, 'seq', axis=0, tiled=True)]
    ppermute x0 -> x7, waiting for transfers between devices: none -> 39.5 us  [the longest x4 39.5 us: collect(): from_left = lax.ppermute(from_left, axis, upward)]
    dynamic_update_slice x0 -> x7, local copies, waits for them, and re-layouts: none -> 9.91 us  [the longest x4 5.47 us: collect(): lax.dynamic_update_slice_in_dim(result, from_left, (index - step) % devic...]
    ppermute x0 -> x7, starting transfers between devices: none -> 9.03 us  [the longest x3 9.02 us: collect(): from_right = lax.ppermute(from_right, axis, left)]
  transfers between devices with their start and end apart: 6 -> 12, of which waited for: 6 -> 9; matrix products, arithmetic and copies ran while one was open for 2% -> 4% of each run, Pallas kernels for 0% -> 0%
where the time goes in v1:
time: 565 us; the launch traced here: 564 us
  waiting for transfers between devices  265 us (47%)
  blocking collectives  145 us (26%)
  matrix products  55.6 us (10%)
  local copies, waits for them, and re-layouts  46.4 us (8%)
  other arithmetic  21.2 us (4%)
  starting transfers between devices  17.4 us (3%)
  between operations  13.5 us (2%)
    all_to_all x2, blocking collectives, sum_at_owner(): tiles = lax.all_to_all(cut_along(x, dim, devices), axis, 0, 0, tiled=True)  88.6 us
    reduce_scatter x1, waiting for transfers between devices, local(): lax.psum_scatter(jnp.dot(picked, weight_flat, preferred_element_type=jnp....  82.4 us
    reduce_scatter x2, waiting for transfers between devices, sum_by_axis(): nearer = lax.psum_scatter(x, axes[0], scatter_dimension=dim, tiled=True)  66.5 us
    all_to_all x2, blocking collectives, from_everyone(): return lax.all_to_all(copies, axis, split_axis=0, concat_axis=0, tiled=True)  45 us
    ppermute x4, waiting for transfers between devices, collect(): from_left = lax.ppermute(from_left, axis, upward)  39.5 us
    all_gather x1, waiting for transfers between devices, local(): gathered = lax.all_gather(blocks, TP, axis=0, tiled=True)  39.4 us
    all_to_all x1, waiting for transfers between devices, from_everyone(): return lax.all_to_all(copies, axis, split_axis=0, concat_axis=0, tiled=True)  36.8 us
    dot_general x1, matrix products, local(): jnp.dot(picked, weight_flat, preferred_element_type=jnp.float32)  22.3 us
  transfers between devices with their start and end apart: 12, of which 9 were waited for; matrix products, arithmetic and copies ran while one was open for 4% of the time, Pallas kernels for 0%

profile of v1, /device:TPU:0, one launch (start us, length us, event | category | flops | bytes accessed | tf_op | source)
XLA Modules:
  0.0 563.9 jit_solution(9632567118443035827)
XLA Ops:
  11.7 8.2 %all-to-all-start = ((bf16[16,64,1280]{2,1,0:T(8,128)(2,1)}), bf16[16,64,1280]{2,1,0:T(8,128)(2,1)}, u32[]{:S(2)}, u32[]{:S(2)}) async-start(bf16[16,64,1280]{2,1,0:T(8,128)(2,1)} %broadcast_in_dim.48), calls=%async_computation | async-start | bytes 5242880 | tf_op jit(solution)/shard_map/all_to_all | solution.py:36
  20.3 36.8 %all-to-all-done = bf16[16,64,1280]{2,1,0:T(8,128)(2,1)} async-done(((bf16[16,64,1280]{2,1,0:T(8,128)(2,1)}), bf16[16,64,1280]{2,1,0:T(8,128)(2,1)}, u32[]{:S(2)}, u32[]{:S(2)}) %all-to-all-start) | async-done | bytes 2621472 | tf_op jit(solution)/shard_map/all_to_all | solution.py:36
  63.6 6.0 %convolution_convert_fusion.2 = bf16[1024,1280]{1,0:T(8,128)(2,1)} fusion(bf16[80,1280]{1,0:T(8,128)(2,1)S(1)} %copy-done.9, f32[1024,1024]{0,1:T(8,128)} %copy-done.4, f32[1024]{0:T(1024)S(1)} %fusion.3, f32[1024]{0:T(1024)S(1)} %get-tuple-element.7, s32[1024]{0:T(1024)S(1)} %fusion.57, bf16[1024,3,1,80]{0,3,1,2:T(8,128)(2,1)} %bitcast.64), kind=kOutput, calls=%fused_computation.14 | convolution fusion | flops 385171456 | bytes 7200768 | tf_op jit(solution)/shard_map/dot_general | solution.py:137
  69.6 37.0 %all_to_all.45 = bf16[16,64,1280]{2,1,0:T(8,128)(2,1)S(1)} all-to-all(bf16[16,64,1280]{2,1,0:T(8,128)(2,1)} %bitcast.55), channel_id=1, replica_groups=mesh['seq'=8,'tp_0'=4,'tp_1'=4] {'tp_0','tp_1'}, dimensions={0} | all-to-all | bytes 5242880 | tf_op jit(solution)/shard_map/all_to_all | solution.py:57
  109.5 35.3 %all_to_all.46 = bf16[16,16,5120]{2,1,0:T(8,128)(2,1)} all-to-all(bf16[16,16,5120]{2,1,0:T(8,128)(2,1)S(1)} %broadcast_in_dim.50), channel_id=1, replica_groups=mesh['seq'=8,'tp_0'=4,'tp_1'=4] {'tp_0','tp_1'}, dimensions={0} | all-to-all | bytes 5242880 | tf_op jit(solution)/shard_map/all_to_all | solution.py:36
  144.8 10.9 %convolution_convert_fusion.1 = bf16[256,8192]{1,0:T(8,128)(2,1)} fusion(bf16[320,8192]{1,0:T(8,128)(2,1)} %param.20, bf16[256,5120]{1,0:T(8,128)(2,1)} %bitcast.56, bf16[5120,320]{0,1:T(8,128)(2,1)S(1)} %copy-done), kind=kOutput, calls=%fused_computation.3 | convolution fusion | flops 2188460032 | bytes 15335424 | tf_op jit(solution)/shard_map/dot_general | solution.py:152
  155.7 51.6 %all_to_all.47 = bf16[16,16,8192]{2,1,0:T(8,128)(2,1)} all-to-all(bf16[16,16,8192]{2,1,0:T(8,128)(2,1)} %bitcast.54), channel_id=1, replica_groups=mesh['seq'=8,'tp_0'=4,'tp_1'=4] {'tp_0','tp_1'}, dimensions={0} | all-to-all | bytes 8388608 | tf_op jit(solution)/shard_map/all_to_all | solution.py:57
  210.2 11.7 %all_to_all.48 = bf16[16,8,1024]{2,0,1:T(8,128)(2,1)} all-to-all(bf16[16,8,1024]{2,0,1:T(8,128)(2,1)S(1)} %bitcast.59), channel_id=1, replica_groups=mesh['seq'=8,'tp_0'=4,'tp_1'=4] {'seq'}, dimensions={1} | all-to-all | bytes 524288 | tf_op jit(solution)/shard_map/all_to_all | solution.py:154
  222.0 8.0 %scatter_custom_fusion = s32[2048]{0:T(1024)S(1)} fusion(s32[2048]{0:T(1024)S(1)} %compare_select_fusion.1, s32[2048]{0:T(1024)S(1)} %iota.7, s32[]{:T(128)} %constant.57.clone.1), kind=kCustom, calls=%fused_computation.97 | custom fusion | bytes 8196 | tf_op jit(solution)/shard_map/scatter | solution.py:101
  230.1 39.4 %all-gather.2.cloned.1.call-done = bf16[2048,1024]{1,0:T(8,128)(2,1)} async-done(((bf16[128,1024]{1,0:T(8,128)(2,1)}), bf16[2048,1024]{1,0:T(8,128)(2,1)}) %all-gather.2.cloned.1.call-update) | async-done | bytes 4194320 | tf_op jit(solution)/shard_map/all_gather | solution.py:155
  269.6 5.0 copy.21
  274.6 13.7 %gather_fusion = bf16[2048,1024]{1,0:T(8,128)(2,1)} fusion(bf16[2048,1024]{1,0:T(8,128)(2,1)} %bitcast.52, s32[2048]{0:T(1024)S(1)} %fusion.58), kind=kCustom, calls=%fused_computation | custom fusion | bytes 8396800 | tf_op jit(solution)/shard_map/jit(_take)/gather | solution.py:163
  288.2 3.1 multiply_reduce_fusion
  291.4 9.7 %all_to_all.49 = f32[8,1,2048]{2,1,0:T(1,128)S(1)} all-to-all(f32[8,1,2048]{2,1,0:T(1,128)S(1)} %broadcast_in_dim.54), channel_id=1, replica_groups=mesh['seq'=8,'tp_0'=4,'tp_1'=4] {'seq'}, dimensions={0} | all-to-all | bytes 131072 | tf_op jit(solution)/shard_map/all_to_all | solution.py:36
  301.1 22.3 %convolution_convert_fusion = bf16[2048,3696]{0,1:T(8,128)(2,1)} fusion(bf16[1024,3696]{0,1:T(8,128)(2,1)} %bitcast.60, f32[1024]{0:T(1024)S(1)} %copy-done.10, f32[2048]{0:T(1024)S(1)} %add_rsqrt_fusion, bf16[2048,1024]{1,0:T(8,128)(2,1)} %gather_fusion, pred[2048]{0:T(1024)(128)(4,1)S(1)} %compare_and_fusion), kind=kOutput, calls=%fused_computation.2 | convolution fusion | flops 15520202752 | bytes 26916864 | tf_op jit(solution)/shard_map/dot_general | solution.py:174
  323.5 82.4 %reduce-scatter.4.cloned.1.call-done = bf16[256,3696]{0,1:T(8,128)(2,1)} async-done(((bf16[2048,3696]{0,1:T(8,128)(2,1)}), bf16[256,3696]{0,1:T(8,128)(2,1)}) %reduce-scatter.4.cloned.1.call-update) | async-done | bytes 1892368 | tf_op jit(solution)/shard_map/reduce_scatter | solution.py:173
  415.3 11.4 %collective-permute-done = bf16[256,1848]{0,1:T(8,128)(2,1)S(1)} collective-permute-done((bf16[256,1848]{0,1:T(8,128)(2,1)S(1)}, bf16[256,1848]{0,1:T(8,128)(2,1)S(1)}, u32[]{:S(2)}, u32[]{:S(2)}) %collective-permute-start) | collective-permute-done | bytes 946208 | tf_op jit(solution)/shard_map/ppermute | solution.py:22
  429.7 11.3 %collective-permute-done.2 = bf16[256,1848]{0,1:T(8,128)(2,1)S(1)} collective-permute-done((bf16[256,1848]{0,1:T(8,128)(2,1)S(1)}, bf16[256,1848]{0,1:T(8,128)(2,1)S(1)}, u32[]{:S(2)}, u32[]{:S(2)}) %collective-permute-start.2) | collective-permute-done | bytes 946208 | tf_op jit(solution)/shard_map/ppermute | solution.py:22
  448.5 6.8 %collective-permute-done.4 = bf16[256,1848]{0,1:T(8,128)(2,1)S(1)} collective-permute-done((bf16[256,1848]{0,1:T(8,128)(2,1)S(1)}, bf16[256,1848]{0,1:T(8,128)(2,1)S(1)}, u32[]{:S(2)}, u32[]{:S(2)}) %collective-permute-start.4) | collective-permute-done | bytes 946208 | tf_op jit(solution)/shard_map/ppermute | solution.py:22
  459.7 10.0 %collective-permute-done.6 = bf16[256,1848]{0,1:T(8,128)(2,1)S(1)} collective-permute-done((bf16[256,1848]{0,1:T(8,128)(2,1)S(1)}, bf16[256,1848]{0,1:T(8,128)(2,1)S(1)}, u32[]{:S(2)}, u32[]{:S(2)}) %collective-permute-start.6) | collective-permute-done | bytes 946208 | tf_op jit(solution)/shard_map/ppermute | solution.py:22
  470.8 12.8 %convolution_convert_fusion.3 = bf16[2048,1024]{1,0:T(8,128)(2,1)} fusion(bf16[2048,1848]{0,1:T(8,128)(2,1)} %constant_dynamic-update-slice_fusion, bf16[1848,1024]{1,0:T(8,128)(2,1)S(1)} %copy-done.8), kind=kOutput, calls=%fused_computation.15 | convolution fusion | flops 7753170944 | bytes 15548416 | tf_op jit(solution)/shard_map/dot_general | solution.py:182
  483.7 45.8 %reduce-scatter.6.cloned.1.call-done = bf16[512,1024]{1,0:T(8,128)(2,1)} async-done(((bf16[2048,1024]{1,0:T(8,128)(2,1)}), bf16[512,1024]{1,0:T(8,128)(2,1)}) %reduce-scatter.6.cloned.1.call-update) | async-done | bytes 1048592 | tf_op jit(solution)/shard_map/reduce_scatter | solution.py:69
  529.5 5.3 fusion.95
  534.8 20.6 %reduce-scatter.8.cloned.1.call-done = bf16[128,1024]{1,0:T(8,128)(2,1)} async-done(((bf16[512,1024]{1,0:T(8,128)(2,1)}), bf16[128,1024]{1,0:T(8,128)(2,1)}) %reduce-scatter.8.cloned.1.call-update) | async-done | bytes 262160 | tf_op jit(solution)/shard_map/reduce_scatter | solution.py:69
  (84 shorter events, 45.3 us)
Async XLA Ops:
  6.5 138.2 %copy-start = (bf16[5120,320]{0,1:T(8,128)(2,1)S(1)}, bf16[5120,320]{0,1:T(8,128)(2,1)}, u32[]{:S(2)}) copy-start(bf16[5120,320]{0,1:T(8,128)(2,1)} %param.19) | copy-start | bytes 9830404
  8.9 11.1 %copy-start.11 = (s32[1,2]{1,0:T(1,128)S(1)}, s32[1,2]{1,0:T(1,128)}, u32[]{:S(2)}) copy-start(s32[1,2]{1,0:T(1,128)} %param.13) | copy-start | bytes 28
  11.7 45.3 %all-to-all-start = ((bf16[16,64,1280]{2,1,0:T(8,128)(2,1)}), bf16[16,64,1280]{2,1,0:T(8,128)(2,1)}, u32[]{:S(2)}, u32[]{:S(2)}) async-start(bf16[16,64,1280]{2,1,0:T(8,128)(2,1)} %broadcast_in_dim.48), calls=%async_computation | async-start | bytes 5242880 | tf_op jit(solution)/shard_map/all_to_all | solution.py:36
  19.9 249.6 %all-gather.2.cloned.1.call-start = ((), (), s32[]{:S(2)}) async-start(), calls=%async_computation.9 | async-start | bytes 4456448 | tf_op jit(solution)/shard_map/all_gather | solution.py:155
  59.8 3.8 copy-start.9
  60.7 1.9 copy-start.4
  69.6 37.4 %copy-start.3 = (bf16[64,1280]{1,0:T(8,128)(2,1)S(1)}, bf16[64,1280]{1,0:T(8,128)(2,1)}, u32[]{:S(2)}) copy-start(bf16[64,1280]{1,0:T(8,128)(2,1)} %param.12) | copy-start | bytes 491524
  69.6 37.7 %copy-start.7 = (f32[1280]{0:T(1024)S(1)}, f32[1280]{0:T(1024)}, u32[]{:S(2)}) copy-start(f32[1280]{0:T(1024)} %param.18) | copy-start | bytes 15364
  207.3 14.7 %copy-start.6 = (s32[2048]{0:T(1024)S(1)}, s32[2048]{0:T(1024)}, u32[]{:S(2)}) copy-start(s32[2048]{0:T(1024)} %param.14) | copy-start | bytes 24580
  222.0 184.0 %reduce-scatter.4.cloned.1.call-start = ((), (), s32[]{:S(2)}) async-start(), calls=%async_computation.10 | async-start | bytes 17031168 | tf_op jit(solution)/shard_map/reduce_scatter | solution.py:173
  288.2 12.9 %copy-start.10 = (f32[1024]{0:T(1024)S(1)}, f32[1024]{0:T(1024)}, u32[]{:S(2)}) copy-start(f32[1024]{0:T(1024)} %param.21) | copy-start | bytes 12292
  323.5 206.0 %reduce-scatter.6.cloned.1.call-start = ((), (), s32[]{:S(2)}) async-start(), calls=%async_computation.11 | async-start | bytes 5242880 | tf_op jit(solution)/shard_map/reduce_scatter | solution.py:69
  409.3 3.0 copy-start.2
  412.3 14.3 %collective-permute-start = (bf16[256,1848]{0,1:T(8,128)(2,1)S(1)}, bf16[256,1848]{0,1:T(8,128)(2,1)S(1)}, u32[]{:S(2)}, u32[]{:S(2)}) collective-permute-start(bf16[256,1848]{0,1:T(8,128)(2,1)S(1)} %get-tuple-element.6), channel_id=1, source_target_pairs={{0,16},{16,32},{32,48},{48,64},{64,80},{80,96},{96,112},{112,0},{1... | collective-permute-start | bytes 2838536 | tf_op jit(solution)/shard_map/ppermute | solution.py:22
  412.3 14.3 %collective-permute-start.1 = (bf16[256,1848]{0,1:T(8,128)(2,1)S(1)}, bf16[256,1848]{0,1:T(8,128)(2,1)}, u32[]{:S(2)}, u32[]{:S(2)}) collective-permute-start(bf16[256,1848]{0,1:T(8,128)(2,1)S(1)} %get-tuple-element.6), channel_id=1, source_target_pairs={{0,112},{16,0},{32,16},{48,32},{64,48},{80,64},{96,80},{112,96},{1... | collective-permute-start | bytes 2838536 | tf_op jit(solution)/shard_map/ppermute | solution.py:27
  426.7 14.3 %copy-start.5 = (bf16[256,1848]{0,1:T(8,128)(2,1)}, bf16[256,1848]{0,1:T(8,128)(2,1)S(1)}, u32[]{:S(2)}) copy-start(bf16[256,1848]{0,1:T(8,128)(2,1)S(1)} %collective-permute-done) | copy-start | bytes 2838532
  426.7 14.3 %collective-permute-start.2 = (bf16[256,1848]{0,1:T(8,128)(2,1)S(1)}, bf16[256,1848]{0,1:T(8,128)(2,1)S(1)}, u32[]{:S(2)}, u32[]{:S(2)}) collective-permute-start(bf16[256,1848]{0,1:T(8,128)(2,1)S(1)} %collective-permute-done), channel_id=1, source_target_pairs={{0,16},{16,32},{32,48},{48,64},{64,80},{80,96},{96,112},{112,0},{1... | collective-permute-start | bytes 2838536 | tf_op jit(solution)/shard_map/ppermute | solution.py:22
  426.7 16.6 %collective-permute-start.3 = (bf16[256,1848]{0,1:T(8,128)(2,1)}, bf16[256,1848]{0,1:T(8,128)(2,1)S(1)}, u32[]{:S(2)}, u32[]{:S(2)}) collective-permute-start(bf16[256,1848]{0,1:T(8,128)(2,1)} %collective-permute-done.1), channel_id=1, source_target_pairs={{0,112},{16,0},{32,16},{48,32},{64,48},{80,64},{96,80},{112,96},{1... | collective-permute-start | bytes 2838536 | tf_op jit(solution)/shard_map/ppermute | solution.py:27
  441.0 14.3 %collective-permute-start.4 = (bf16[256,1848]{0,1:T(8,128)(2,1)S(1)}, bf16[256,1848]{0,1:T(8,128)(2,1)S(1)}, u32[]{:S(2)}, u32[]{:S(2)}) collective-permute-start(bf16[256,1848]{0,1:T(8,128)(2,1)S(1)} %collective-permute-done.2), channel_id=1, source_target_pairs={{0,16},{16,32},{32,48},{48,64},{64,80},{80,96},{96,112},{112,0},{1... | collective-permute-start | bytes 2838536 | tf_op jit(solution)/shard_map/ppermute | solution.py:22
  443.3 15.3 %collective-permute-start.5 = (bf16[256,1848]{0,1:T(8,128)(2,1)S(1)}, bf16[256,1848]{0,1:T(8,128)(2,1)S(1)}, u32[]{:S(2)}, u32[]{:S(2)}) collective-permute-start(bf16[256,1848]{0,1:T(8,128)(2,1)S(1)} %collective-permute-done.3), channel_id=1, source_target_pairs={{0,112},{16,0},{32,16},{48,32},{64,48},{80,64},{96,80},{112,96},{1... | collective-permute-start | bytes 2838536 | tf_op jit(solution)/shard_map/ppermute | solution.py:27
  455.3 14.3 %collective-permute-start.6 = (bf16[256,1848]{0,1:T(8,128)(2,1)S(1)}, bf16[256,1848]{0,1:T(8,128)(2,1)S(1)}, u32[]{:S(2)}, u32[]{:S(2)}) collective-permute-start(bf16[256,1848]{0,1:T(8,128)(2,1)S(1)} %collective-permute-done.4), channel_id=1, source_target_pairs={{0,16},{16,32},{32,48},{48,64},{64,80},{80,96},{96,112},{112,0},{1... | collective-permute-start | bytes 2838536 | tf_op jit(solution)/shard_map/ppermute | solution.py:22
  456.5 14.3 %copy-start.8 = (bf16[1848,1024]{1,0:T(8,128)(2,1)S(1)}, bf16[1848,1024]{1,0:T(8,128)(2,1)}, u32[]{:S(2)}) copy-start(bf16[1848,1024]{1,0:T(8,128)(2,1)} %param.23) | copy-start | bytes 11354116
  483.6 71.9 %reduce-scatter.8.cloned.1.call-start = ((), (), s32[]{:S(2)}) async-start(), calls=%async_computation.12 | async-start | bytes 1310720 | tf_op jit(solution)/shard_map/reduce_scatter | solution.py:69
  529.5 27.8 %copy-start.1 = (bf16[5120,320]{0,1:T(8,128)(2,1)S(1)}, bf16[5120,320]{0,1:T(8,128)(2,1)}, u32[]{:S(2)}) copy-start(bf16[5120,320]{0,1:T(8,128)(2,1)} %param.19) | copy-start | bytes 9830404
  (1 other events, 0.9 us)
Sparse Core Ops, SparseCore 0:
  222.1 47.4 all-gather.1
  323.6 82.2 reduce-scatter.3
  483.7 45.7 reduce-scatter.5
  531.7 23.6 reduce-scatter.7
